TPU v7x, 8 devices: a whole 2x2x1 slice. The times are simulated.
8 devices in a mesh: data: 1 (over z), cp: 2 (over y), tp: 4 (over x, core).
Axes of the slice: x: 2, y: 2, z: 1, core: 2. Of those that a mesh axis runs over, the one named last changes fastest.
Arguments:
- x_in: bfloat16 [4096, 2048], P(('data', 'cp', 'tp'))
- w_q: bfloat16 [2048, 32, 128], P(None, 'tp')
- w_k: bfloat16 [2048, 4, 128], P(None, 'tp')
- w_v: bfloat16 [2048, 4, 128], P(None, 'tp')
- w_o: bfloat16 [32, 128, 2048], P('tp')
- expert_idx: int32 [4096, 2], P(('data', 'cp', 'tp'))
- gate_wts: float32 [4096, 2], P(('data', 'cp', 'tp'))
- w_gate: bfloat16 [128, 2048, 768], P(('cp', 'tp'))
- w_up: bfloat16 [128, 2048, 768], P(('cp', 'tp'))
- w_down: bfloat16 [128, 768, 2048], P(('cp', 'tp'))
Outputs:
- output: bfloat16 [4096, 2048], P(('data', 'cp', 'tp'))
All inputs are finite; a program needn't handle non-finite values.
Results may differ from a plain program's by a relative error of at most 0.0146991.
Values are sent between devices in bfloat16 or wider.
A program may use at most 1 GiB of HBM per device.

v0:
```python
import functools
import jax
import jax.numpy as jnp
from jax import lax
from jax.experimental import pallas as pl
from jax.experimental.pallas import tpu as pltpu
from jax.sharding import PartitionSpec as P

QB = 256
KB = 512
CH = 128
HC = 64
OVER_X = (7,)
OV = 32
LIMIT = OV
WR = 256
LOG2E = 1.4426950408889634
VLIM = 60 * 1024 * 1024
MESH = pl.DeviceIdType.MESH


def attend_block(q_of, kv_ref, m_ref, l_ref, acc_ref, pos0, heads, hd):
    c = (hd ** -0.5) * LOG2E
    m_ref[...] = jnp.full(m_ref.shape, -jnp.inf, jnp.float32)
    l_ref[...] = jnp.zeros(l_ref.shape, jnp.float32)
    acc_ref[...] = jnp.zeros(acc_ref.shape, jnp.float32)

    def step(kb, masked):
        start = pl.multiple_of(kb * KB, KB)
        k = kv_ref[pl.ds(start, KB), :hd]
        v = kv_ref[pl.ds(start, KB), hd:]
        score = lambda h: lax.dot_general(q_of(h), k, (((1,), (1,)), ((), ())), preferred_element_type=jnp.float32)
        if masked:
            qp = pos0 + lax.broadcasted_iota(jnp.int32, (QB, KB), 0)
            kp = start + lax.broadcasted_iota(jnp.int32, (QB, KB), 1)
            keep = kp <= qp
        s_next = score(0)
        for h in range(heads):
            rows = slice(h * QB, (h + 1) * QB)
            s = s_next
            if h + 1 < heads:
                s_next = score(h + 1)
            if masked:
                s = jnp.where(keep, s, -jnp.inf)
            m_old = m_ref[rows, :]
            m_new = jnp.maximum(m_old, jnp.max(s, axis=1, keepdims=True))
            alpha = jnp.exp2((m_old - m_new) * c)
            p = jnp.exp2((s - jnp.concatenate([m_new] * (KB // 128), axis=1)) * c)
            lp = p[:, :128]
            for j in range(1, KB // 128):
                lp = lp + p[:, j * 128:(j + 1) * 128]
            m_ref[rows, :] = m_new
            l_ref[rows, :] = l_ref[rows, :] * alpha + lp
            acc_ref[rows, :] = acc_ref[rows, :] * alpha + jnp.dot(p.astype(jnp.bfloat16), v, preferred_element_type=jnp.float32)

    last = pos0 // KB

    def body(kb, carry):
        step(kb, False)
        return carry

    lax.fori_loop(0, last, body, 0)
    step(last, True)


def rdma(src, dst, send_sem, recv_sem, cp, tp):
    return pltpu.make_async_remote_copy(src_ref=src, dst_ref=dst, send_sem=send_sem, recv_sem=recv_sem, device_id=(0, cp, tp), device_id_type=MESH)


def await_bytes(ref, sem):
    pltpu.make_async_copy(ref, ref, sem).wait()


def greet(others):
    barrier = pltpu.get_barrier_semaphore()
    for cp, tp in others:
        pl.semaphore_signal(barrier, inc=1, device_id=(0, cp, tp), device_id_type=MESH)
    pl.semaphore_wait(barrier, len(others))


def slot_rows(idx_ref, num_exp, exp_local, cap):
    rows = idx_ref.shape[1]
    expert = lax.broadcasted_iota(jnp.int32, (num_exp, rows), 0)
    hot = [jnp.where(idx_ref[k:k + 1, :] == expert, 1.0, 0.0) for k in range(2)]
    earlier = lax.broadcasted_iota(jnp.int32, (rows, rows), 0) < lax.broadcasted_iota(jnp.int32, (rows, rows), 1)
    earlier = jnp.where(earlier, 1.0, 0.0).astype(jnp.bfloat16)
    count = jnp.dot((hot[0] + hot[1]).astype(jnp.bfloat16), earlier, preferred_element_type=jnp.float32)
    lane_sum = jnp.sum(hot[0] + hot[1], axis=1, keepdims=True)
    over = jnp.maximum(lane_sum - cap // 2, 0.0)
    e0 = lax.broadcasted_iota(jnp.int32, (num_exp, num_exp), 0)
    e1 = lax.broadcasted_iota(jnp.int32, (num_exp, num_exp), 1)
    before = jnp.where(jnp.logical_and(e0 // exp_local == e1 // exp_local, e1 < e0), 1.0, 0.0).astype(jnp.bfloat16)
    offset = jnp.dot(before, jnp.broadcast_to(over, (num_exp, num_exp)).astype(jnp.bfloat16), preferred_element_type=jnp.float32)[:, 0:1]
    worst = jnp.broadcast_to(jnp.max(offset + over, axis=0, keepdims=True), (1, rows)).astype(jnp.int32)
    slots, ranks = [], []
    for k in range(2):
        pos = jnp.sum(hot[k] * count, axis=0, keepdims=True)
        rank = jnp.sum(hot[k] * offset, axis=0, keepdims=True) + pos - cap // 2
        slots.append(idx_ref[k:k + 1, :] * cap + pos.astype(jnp.int32))
        ranks.append(jnp.where(pos >= cap // 2, rank, -1.0).astype(jnp.int32))
    return slots + ranks + [worst]


def front_kernel(cp_size, tp_size, heads, hd, num_exp, cap, x_ref, idx_ref, wq_ref, wk_ref, wv_ref, wo_ref, h_ref, tok_ref, hbuf, own_slots, slots,
                 x_all, wq, wkv, wo, q_ref, kv_ref, m_ref, l_ref, acc_ref, ob_ref, part, from_near, from_far,
                 wsem, slot_send, slot_recv, x_send, x_near, x_far, x_fwd_send, x_fwd, kv_send, kv_recv,
                 near_send, near_recv, far_send, far_recv, h_send, h_near, h_far, h_peer, h_diag, load_sem, tok_sem, raw, raw_sem):
    r, t = lax.axis_index('cp'), lax.axis_index('tp')
    num_devs = cp_size * tp_size
    me = r * tp_size + t
    near = t + 1 - 2 * lax.rem(t, 2)
    far = lax.rem(t + 2, tp_size)
    far_near = lax.rem(near + 2, tp_size)
    peer = 1 - r
    rows, width = x_ref.shape
    half_rows = rows // 2
    devs = [lax.rem(me + j, num_devs) for j in range(1, num_devs)]

    weights = [pltpu.make_async_copy(wk_ref, wkv.at[:, pl.ds(0, hd)], wsem.at[0]), pltpu.make_async_copy(wv_ref, wkv.at[:, pl.ds(hd, hd)], wsem.at[1]), pltpu.make_async_copy(wo_ref, wo, wsem.at[2])]
    for copy in weights:
        copy.start()

    def raw_copy(k, slot):
        return pltpu.make_async_copy(wq_ref.at[pl.ds(pl.multiple_of(k * WR, WR), WR)], raw.at[slot], raw_sem.at[slot])

    for k in range(2):
        raw_copy(k, k).start()
    greet([(d // tp_size, lax.rem(d, tp_size)) for d in devs])
    chunks = rows // CH
    for j in range(chunks):
        at = pl.ds(j * CH, CH)
        rdma(x_ref.at[at], x_all.at[0, at], x_send, x_far.at[j], r, far).start()
    rdma(x_ref, x_all.at[1], x_send, x_near, r, near).start()
    mine = slot_rows(idx_ref, num_exp, num_exp // num_devs, cap)
    own_slots[...] = jnp.concatenate(mine + [jnp.zeros((3, rows), jnp.int32)], axis=0)
    slots[me] = own_slots[...]
    for d in devs:
        rdma(own_slots, slots.at[me], slot_send, slot_recv, d // tp_size, lax.rem(d, tp_size)).start()
    for copy in weights[:2]:
        copy.wait()

    def flatten(k, carry):
        slot = lax.rem(k, 2)
        raw_copy(k, slot).wait()
        at = pl.ds(pl.multiple_of(k * WR, WR), WR)
        for h in range(heads):
            wq[at, h * hd:(h + 1) * hd] = raw[slot, :, h, :]

        @pl.when(k + 2 < width // WR)
        def _():
            raw_copy(k + 2, slot).start()

        return carry

    lax.fori_loop(0, width // WR, flatten, 0)

    def project(x, tp_src, row0, count):
        half = row0 // half_rows
        seg = r + half * (2 * cp_size - 1 - 2 * r)
        pos = pl.multiple_of((seg * tp_size + tp_src) * half_rows + row0 % half_rows, CH)
        kv_ref[pl.ds(pos, count), :] = jnp.dot(x, wkv[...], preferred_element_type=jnp.float32).astype(jnp.bfloat16)
        sent = kv_ref.at[pl.ds(pos, count)]
        rdma(sent, sent, kv_send, kv_recv.at[half], peer, t).start()
        at = pl.ds(pl.multiple_of(tp_src * rows + row0, CH), count)
        q_ref[at, :] = jnp.dot(x, wq[...], preferred_element_type=jnp.float32).astype(jnp.bfloat16)

    def project_far(half):
        def chunk(j, carry):
            first = pl.multiple_of(j * CH, CH)
            at = pl.ds(first, CH)
            await_bytes(x_all.at[0, at], x_far.at[j])
            rdma(x_all.at[0, at], x_all.at[2, at], x_fwd_send, x_fwd.at[j], r, near).start()
            project(x_all[0, at, :], far, first, CH)
            await_bytes(x_all.at[2, at], x_fwd.at[j])
            project(x_all[2, at, :], far_near, first, CH)
            return carry

        lax.fori_loop(half * (chunks // 2), (half + 1) * (chunks // 2), chunk, 0)
        await_bytes(kv_ref.at[pl.ds(0, tp_size * half_rows)], kv_recv.at[half])

    def project_half(x_at, tp_src):
        def step(half, carry):
            first = pl.multiple_of(half * half_rows, half_rows)
            project(x_at[pl.ds(first, half_rows), :], tp_src, first, half_rows)
            return carry

        lax.fori_loop(0, 2, step, 0)

    project_half(x_ref, t)
    await_bytes(x_all.at[1], x_near)
    project_half(x_all.at[1], near)
    project_far(0)
    weights[2].wait()

    def h_rows(cp, tp, j):
        return h_ref.at[pl.ds(pl.multiple_of((cp * tp_size + tp) * rows + j * HC, HC), HC)]

    def h_block(cp, tp):
        return h_ref.at[pl.ds(pl.multiple_of((cp * tp_size + tp) * rows, rows), rows)]

    OWN, PEER, FAR, DIAG = range(4)
    h_chunks = rows // HC

    def finish(half):
        await_bytes(from_near.at[2 + half], near_recv.at[2 + half])
        for within in range(0, QB, HC):
            first = half * QB + within
            j = first // HC
            at = slice(within, within + HC)
            if within % CH == 0:
                await_bytes(from_far.at[half, pl.ds(within, CH)], far_recv.at[half, within // CH])
            total = part[4 + half, at, :] + from_near[2 + half, at, :] + from_far[half, at, :]
            hbuf[first:first + HC, :] = (x_ref[first:first + HC, :].astype(jnp.float32) + total).astype(jnp.bfloat16)
            src = hbuf.at[pl.ds(first, HC)]
            mine = h_rows(r, t, j)
            rdma(src, mine, h_send, h_far.at[j], r, far).start()
            rdma(src, mine, h_send, h_peer.at[j], peer, t).start()
            rdma(src, mine, h_send, h_near.at[OWN], r, near).start()

    def forward(got, kind):
        rdma(got, got, h_send, h_near.at[kind], r, near).start()

    def diag(j):
        got = h_rows(peer, far, j)
        await_bytes(got, h_diag.at[j])
        forward(got, DIAG)

    def from_peer(j):
        got = h_rows(peer, t, j)
        await_bytes(got, h_peer.at[j])
        forward(got, PEER)
        if j in OVER_X:
            rdma(got, got, h_send, h_diag.at[j], r, far).start()

    def across(j):
        got = h_rows(r, far, j)
        await_bytes(got, h_far.at[j])
        forward(got, FAR)
        if j not in OVER_X:
            rdma(got, got, h_send, h_diag.at[j], peer, t).start()

    def block(i, carry):
        half = i // 4
        local = lax.rem(i // 2, 2)
        mine = lax.rem(i, 2)
        slot = mine * (2 + 2 * local) + half

        @pl.when(i == 4)
        def _():
            project_far(1)

        @pl.when(i == 5)
        def _():
            finish(0)

        @pl.when(i == 7)
        def _():
            for j in range(h_chunks // 2):
                from_peer(j)
            for j in range(h_chunks // 2):
                across(j)

        @pl.when(jnp.logical_and(mine == 0, local == 1))
        def _():
            await_bytes(part.at[half], near_send.at[half])

        t_dst = lax.rem(mine * t + (1 - mine) * near + 2 * (1 - local), tp_size)
        seg = r + half * (2 * cp_size - 1 - 2 * r)
        pos0 = (seg * tp_size + t_dst) * QB
        row0 = pl.multiple_of(t_dst * rows + half * QB, QB)
        attend_block(lambda h: q_ref[pl.ds(row0, QB), h * hd:(h + 1) * hd], kv_ref, m_ref, l_ref, acc_ref, pos0, heads, hd)
        for h in range(heads):
            at = slice(h * QB, (h + 1) * QB)
            den = jnp.sum(l_ref[at, :], axis=1, keepdims=True)
            ob_ref[:, h * hd:(h + 1) * hd] = (acc_ref[at, :] / den).astype(jnp.bfloat16)
        part[slot] = jnp.dot(ob_ref[...], wo[...], preferred_element_type=jnp.float32)

        @pl.when(mine == 0)
        def _():
            rdma(part.at[slot], from_near.at[2 * local + half], near_send.at[half], near_recv.at[2 * local + half], r, near).start()

        @pl.when(jnp.logical_and(mine == 1, local == 0))
        def _():
            await_bytes(from_near.at[half], near_recv.at[half])
            part[slot] += from_near[half]
            for c in range(QB // CH):
                at = pl.ds(c * CH, CH)
                rdma(part.at[slot, at], from_far.at[half, at], far_send, far_recv.at[half, c], r, far).start()

        return carry

    lax.fori_loop(0, 8, block, 0)
    await_bytes(x_all.at[0], x_fwd_send)

    finish(1)
    await_bytes(slots.at[pl.ds(0, num_devs - 1)], slot_recv)
    local_slots = (num_exp // num_devs) * cap

    def pick(pair, ends):
        exp_local = num_exp // num_devs
        sels = []
        for dev, _ in ends:
            ids = slots[dev] - me * local_slots
            want = lax.broadcasted_iota(jnp.int32, (local_slots, rows), 0)
            sel = jnp.logical_or(ids[0:1, :] == want, ids[1:2, :] == want)
            sels.append(jnp.where(sel, 1.0, 0.0).astype(jnp.bfloat16))
        if pair > 0:
            await_bytes(x_all.at[2], tok_sem)
        for c0 in range(0, width, 512):
            parts = [jnp.dot(sel, src[:, c0:c0 + 512], preferred_element_type=jnp.float32).reshape(exp_local, 2, cap // 2, 512) for sel, (_, src) in zip(sels, ends)]
            x_all[2, :, c0:c0 + 512] = jnp.concatenate(parts, axis=2).reshape(rows, 512).astype(jnp.bfloat16)
        for e in range(exp_local):
            for upper in range(2):
                pltpu.make_async_copy(x_all.at[2, pl.ds((2 * e + upper) * cap, cap)], tok_ref.at[e, pl.ds(upper * (num_devs * cap // 2) + pair * cap, cap)], tok_sem).start()

    def fetch(n, cp, tp):
        return pltpu.make_async_copy(h_block(cp, tp), x_all.at[n % 2], load_sem.at[n % 2])

    for j in range(h_chunks // 2):
        diag(j)
    from_peer(4)
    across(4)
    await_bytes(h_block(r, near), h_near.at[OWN])
    fetch(1, r, near).start()
    fetch(1, r, near).wait()
    pick(0, ((me, hbuf), (r * tp_size + near, x_all.at[1])))
    for j in range(5, h_chunks):
        from_peer(j)
        across(j)
    fetch(0, peer, t).start()
    await_bytes(h_block(peer, near), h_near.at[PEER])
    fetch(1, peer, near).start()
    fetch(0, peer, t).wait()
    fetch(1, peer, near).wait()
    pick(1, ((peer * tp_size + t, x_all.at[0]), (peer * tp_size + near, x_all.at[1])))
    fetch(0, r, far).start()
    await_bytes(h_block(r, far_near), h_near.at[FAR])
    fetch(1, r, far_near).start()
    fetch(0, r, far).wait()
    fetch(1, r, far_near).wait()
    pick(2, ((r * tp_size + far, x_all.at[0]), (r * tp_size + far_near, x_all.at[1])))
    for j in range(4, h_chunks):
        diag(j)
    fetch(0, peer, far).start()
    await_bytes(h_block(peer, far_near), h_near.at[DIAG])
    fetch(1, peer, far_near).start()
    fetch(0, peer, far).wait()
    fetch(1, peer, far_near).wait()
    pick(3, ((peer * tp_size + far, x_all.at[0]), (peer * tp_size + far_near, x_all.at[1])))

    await_bytes(x_all.at[2], tok_sem)
    for n in range(2):
        await_bytes(part.at[n], near_send.at[n])
    await_bytes(h_ref.at[pl.ds(0, 7 * rows)], h_send)
    await_bytes(part.at[pl.ds(0, 2)], far_send)
    await_bytes(slots.at[pl.ds(0, num_devs - 1)], slot_send)
    await_bytes(x_all.at[pl.ds(0, 2)], x_send)
    await_bytes(kv_ref.at[pl.ds(0, tp_size * rows)], kv_send)


def moe_kernel(num_devs, tp_size, exp_local, cap, full, tok_ref, h_ref, slot_ref, slots_ref, gate_ref, wg_ref, wu_ref, wd_ref, y_ref, tok, wgb, wub, wdb, zrecv, over, yacc, cols, tsem, wsem, send_sem, over_sem, recv_sem):
    rows, width = y_ref.shape
    r, t = lax.axis_index('cp'), lax.axis_index('tp')
    me = r * tp_size + t
    near = t + 1 - 2 * lax.rem(t, 2)
    places = [(cp, lax.rem(tp + 2 * across, tp_size)) for across in range(2) for cp in (r, 1 - r) for tp in (t, near)]
    low = cap // 2
    pairs = exp_local // 2
    block = num_devs * cap
    half_block = block // 2

    def weight_copies(e, slot):
        return [pltpu.make_async_copy(src.at[e], dst.at[slot], wsem.at[i, slot]) for i, (src, dst) in enumerate(((wg_ref, wgb), (wu_ref, wub), (wd_ref, wdb)))]

    loads = [pltpu.make_async_copy(tok_ref.at[at], tok.at[at], tsem.at[n]) for n, at in enumerate((pl.ds(0, 2), pl.ds(2, exp_local - 2)))]
    for e in range(2):
        loads[e].start()
        for copy in weight_copies(e, e):
            copy.start()
    greet(places[1:])
    slot = slot_ref[0:2, :]
    pos = slot % cap
    expert = slot // cap
    dev = expert // exp_local
    el = expert % exp_local
    dev_cp, dev_tp = dev // tp_size, dev % tp_size
    place = jnp.where(dev_tp % 2 == t % 2, 0, 1) + jnp.where(dev_cp == r, 0, 2) + jnp.where(dev_tp // 2 == t // 2, 0, 4)
    home = (el // 2) * block + place * cap + (el % 2) * low + pos % low
    upper = pairs * block + (home if full else place * OV + slot_ref[2:4, :])
    back = jnp.where(pos < low, home, upper)
    columns = jnp.concatenate([back.astype(jnp.float32), gate_ref[...], jnp.zeros((124, rows), jnp.float32)], axis=0)
    cols[...] = jnp.transpose(columns)
    yacc[...] = h_ref[...].astype(jnp.float32)
    loads[0].wait()

    def send(src, dst, sem, group, n):
        rdma(src, dst, sem, recv_sem.at[group], *places[n]).start()

    def two_experts(m, carry):
        @pl.when(m == 1)
        def _():
            loads[1].wait()

        outs = []
        for b in range(2):
            e = 2 * m + b
            for copy in weight_copies(e, b):
                copy.wait()
            x = tok[e]
            gate = jnp.dot(x, wgb[b], preferred_element_type=jnp.float32)
            up = jnp.dot(x, wub[b], preferred_element_type=jnp.float32)
            act = (jax.nn.silu(gate) * up).astype(jnp.bfloat16)
            outs.append(jnp.dot(act, wdb[b], preferred_element_type=jnp.float32))

            @pl.when(e + 2 < exp_local)
            def _():
                for copy in weight_copies(e + 2, b):
                    copy.start()

        for side in range(2):
            pieces = [z[side * half_block:(side + 1) * half_block].reshape(num_devs, low, width) for z in outs]
            tok[2 * m + side] = jnp.concatenate(pieces, axis=1).reshape(block, width).astype(jnp.bfloat16)
            if side == 0 or full:
                at = side * pairs + m
                for n in range(1, num_devs):
                    part = pl.ds(n * cap, cap)
                    send(tok.at[2 * m + side, part], zrecv.at[at, part], over_sem if side else send_sem, at // 2, n)
                zrecv[at, :cap, :] = tok[2 * m + side, :cap, :]
        return carry

    lax.fori_loop(0, pairs, two_experts, 0)

    if not full:
        per_block = block // OV
        for n in (4, 5, 6, 7, 2, 3, 1, 0):
            cp, tp = places[n]
            ids = slots_ref[cp * tp_size + tp]
            mix = jnp.zeros((OV, half_block), jnp.float32)
            for k in range(2):
                own = ids[k:k + 1, :] - me * exp_local * cap
                inside = jnp.logical_and(own >= 0, own < exp_local * cap)
                spot = jnp.where(jnp.logical_and(inside, own % cap >= low), own // cap * low + own % cap - low, -1)
                a = jnp.where(ids[2 + k:3 + k, :] == lax.broadcasted_iota(jnp.int32, (OV, rows), 0), 1.0, 0.0).astype(jnp.bfloat16)
                b = jnp.where(spot == lax.broadcasted_iota(jnp.int32, (half_block * 2, rows), 0), 1.0, 0.0).astype(jnp.bfloat16)
                mix = lax.dot_general(a, b, (((1,), (1,)), ((), ())), preferred_element_type=jnp.float32) + (mix if k else 0.0)
            mix = mix.astype(jnp.bfloat16)
            for c0 in range(0, width, 512):
                z = jnp.concatenate([tok[2 * m + 1, n * cap:(n + 1) * cap, c0:c0 + 512] for m in range(pairs)], axis=0)
                over[n, :, c0:c0 + 512] = jnp.dot(mix, z, preferred_element_type=jnp.float32).astype(jnp.bfloat16)
            dst = zrecv.at[pairs + n // per_block, pl.ds(n % per_block * OV, OV)]
            if n:
                send(over.at[n], dst, over_sem, pairs // 2, n)
            else:
                dst[...] = over[n]

    groups = recv_sem.shape[0]
    span = 2 * block

    def combine(g, carry):
        await_bytes(zrecv.at[pl.ds(0, 2), pl.ds(0, (num_devs - 1) * cap)], recv_sem.at[g])
        want = (lax.broadcasted_iota(jnp.int32, (rows, span), 1) + g * span).astype(jnp.float32)
        sel0 = jnp.where(cols[:, 0:1] == want, 1.0, 0.0).astype(jnp.bfloat16)
        sel1 = jnp.where(cols[:, 1:2] == want, 1.0, 0.0).astype(jnp.bfloat16)
        first = pl.multiple_of(g * 2, 2)
        for c0 in range(0, width, 512):
            z = zrecv[pl.ds(first, 2), :, c0:c0 + 512].reshape(span, 512)
            z0 = jnp.dot(sel0, z, preferred_element_type=jnp.float32)
            z1 = jnp.dot(sel1, z, preferred_element_type=jnp.float32)
            yacc[:, c0:c0 + 512] += cols[:, 2:3] * z0 + cols[:, 3:4] * z1
        return carry

    lax.fori_loop(0, groups, combine, 0)
    y_ref[...] = yacc[...].astype(y_ref.dtype)
    await_bytes(tok.at[pl.ds(0, pairs), pl.ds(0, (num_devs - 1) * cap)], send_sem)
    await_bytes(tok.at[pl.ds(0, pairs if full else 2), pl.ds(0, (num_devs - 1) * cap)], over_sem)


def solution(mesh):
    cp_size = mesh.shape['cp']
    tp_size = mesh.shape['tp']
    num_devs = cp_size * tp_size
    row_spec = P(('data', 'cp', 'tp'), None)
    head_spec = P(None, 'tp', None)
    wo_spec = P('tp', None, None)
    expert_spec = P(('cp', 'tp'), None, None)

    vmem = pl.BlockSpec(memory_space=pltpu.VMEM)
    hbm = pl.BlockSpec(memory_space=pl.ANY)
    dma = pltpu.SemaphoreType.DMA
    bf16, f32 = jnp.bfloat16, jnp.float32

    def params(number):
        return pltpu.CompilerParams(collective_id=number, has_side_effects=True, vmem_limit_bytes=VLIM)

    def front(x_blk, idx, w_q, w_k, w_v, w_o, heads, hd, exp_local, cap):
        rows, width = x_blk.shape
        group = rows * tp_size
        v32 = lambda *shape: pltpu.VMEM(shape, f32)
        v16 = lambda *shape: pltpu.VMEM(shape, bf16)
        return pl.pallas_call(
            functools.partial(front_kernel, cp_size, tp_size, heads, hd, exp_local * num_devs, cap),
            in_specs=[vmem, vmem, hbm, hbm, hbm, hbm],
            out_specs=[hbm, hbm, vmem, vmem, vmem],
            out_shape=[jax.ShapeDtypeStruct((rows * num_devs, width), bf16), jax.ShapeDtypeStruct((exp_local, num_devs * cap, width), bf16), jax.ShapeDtypeStruct((rows, width), bf16), jax.ShapeDtypeStruct((8, rows), jnp.int32), jax.ShapeDtypeStruct((num_devs, 8, rows), jnp.int32)],
            scratch_shapes=[
                v16(3, rows, width), v16(width, heads * hd), v16(width, 2 * hd), v16(heads * hd, width), v16(group, heads * hd), v16(group * cp_size, 2 * hd),
                v32(heads * QB, 128), v32(heads * QB, 128), v32(heads * QB, hd), v16(QB, heads * hd),
                v32(6, QB, width), v32(4, QB, width), v32(2, QB, width),
                dma((3,)), dma, dma, dma, dma, dma((rows // CH,)), dma, dma((rows // CH,)), dma, dma((2,)),
                dma((2,)), dma((4,)), dma, dma((2, QB // CH)), dma, dma((4,)), dma((rows // HC,)), dma((rows // HC,)), dma((rows // HC,)), dma((2,)), dma, v16(2, WR, heads, hd), dma((2,))],
            compiler_params=params(0),
            name='front',
        )(x_blk, idx, w_q, w_k, w_v, w_o)

    def experts(full, cap, tok, h_own, own_slots, slots, gates, w_gate, w_up, w_down):
        rows, width = h_own.shape
        exp_local, _, ff = w_gate.shape
        v16 = lambda *shape: pltpu.VMEM(shape, bf16)
        block = num_devs * cap
        blocks = exp_local if full else exp_local // 2 + num_devs * OV // block
        return pl.pallas_call(
            functools.partial(moe_kernel, num_devs, tp_size, exp_local, cap, full),
            in_specs=[hbm, vmem, vmem, vmem, vmem, hbm, hbm, hbm],
            out_specs=vmem,
            out_shape=jax.ShapeDtypeStruct((rows, width), bf16),
            scratch_shapes=[v16(exp_local, block, width), v16(2, width, ff), v16(2, width, ff), v16(2, ff, width), v16(blocks, block, width), v16(num_devs, OV, width), pltpu.VMEM((rows, width), f32), pltpu.VMEM((rows, 128), f32), dma((2,)), dma((3, 2)), dma, dma, dma((blocks // 2,))],
            compiler_params=params(2 if full else 1),
            name='moe_full' if full else 'moe',
        )(tok, h_own, own_slots, slots, gates, w_gate, w_up, w_down)

    def device_fn(x_blk, w_q, w_k, w_v, w_o, idx_blk, gate_blk, w_gate, w_up, w_down):
        tok_dev, width = x_blk.shape
        heads, head_dim = w_q.shape[1], w_k.shape[2]
        exp_local = w_gate.shape[0]
        num_exp = exp_local * num_devs
        capacity = 4 * tok_dev // num_exp

        flat = lambda w: w.reshape(width, -1)
        _, tok, h_own, own_slots, slots = front(x_blk, idx_blk.T, w_q, flat(w_k), flat(w_v), w_o.reshape(heads * head_dim, width), heads, head_dim, exp_local, capacity)
        few = jnp.max(slots[:, 4, 0]) <= LIMIT
        return lax.cond(few, functools.partial(experts, False, capacity), functools.partial(experts, True, capacity), tok, h_own, own_slots, slots, gate_blk.T, w_gate, w_up, w_down)

    return jax.shard_map(device_fn, mesh=mesh, in_specs=(row_spec, head_spec, head_spec, head_spec, wo_spec, row_spec, row_spec, expert_spec, expert_spec, expert_spec), out_specs=row_spec, check_vma=False)
```

profile of v0, /device:TPU:0, one launch (start us, length us, event | category | flops | bytes accessed | tf_op | source)
XLA Modules:
  0.0 282.6 jit_solution(16379360824865089161)
XLA Ops:
  0.0 0.0 copy-start
  0.0 204.0 %front.1 = (bf16[4096,2048]{1,0:T(8,128)(2,1)}, bf16[16,128,2048]{2,1,0:T(8,128)(2,1)}, bf16[512,2048]{1,0:T(8,128)(2,1)S(1)}, s32[8,512]{1,0:T(8,128)S(1)}, s32[8,8,512]{2,1,0:T(8,128)S(1)}) custom-call(bf16[512,2048]{1,0:T(8,128)(2,1)} %x_ref.1, s32[2,512]{1,0:T(2,128)} %bitcast.10, bf16[2048,8,128]{2,1,0:T(8,128)(2,1)} %wq_ref.1, ...), custom_call_target="tpu_custom_call" | custom-call | tf_op jit(solution)/shard_map/front/pallas_call | solution.py:500
  204.0 0.6 slice_reduce_fusion
  205.3 0.0 copy-done
  205.3 74.1 %conditional.1 = (bf16[512,2048]{1,0:T(8,128)(2,1)}) conditional(s32[]{:T(128)} %convert_element_type.3, (bf16[16,128,2048]{2,1,0:T(8,128)(2,1)}, bf16[512,2048]{1,0:T(8,128)(2,1)S(1)}, s32[8,512]{1,0:T(8,128)S(1)}, s32[8,8,512]{2,1,0:T(8,128)S(1)}, f32[2,512]{1,0:T(2,128)S(1)}, /*index=5*/bf16[16,2048,768]{2,1,0:T(8,128)(2,1)}, ...), branch_computations={%region_1.0_spmd, %region_2.0_spmd} | conditional | bytes 8 | solution.py:541
  205.4 74.1 %moe.1 = bf16[512,2048]{1,0:T(8,128)(2,1)} custom-call(bf16[16,128,2048]{2,1,0:T(8,128)(2,1)} %get-tuple-element.48.tok_ref, bf16[512,2048]{1,0:T(8,128)(2,1)S(1)} %get-tuple-element.49.h_ref, s32[8,512]{1,0:T(8,128)S(1)} %get-tuple-element.50.slot_ref, s32[8,8,512]{2,1,0:T(8,128)S(1)} %get-tuple-element.51.slots_ref, ...), custom_call_target="tpu_custom_call" | custom-call | tf_op jit(solution)/shard_map/cond/branch_1_fun/moe/pallas_call | solution.py:521
  279.4 3.2 %copy.22 = bf16[512,2048]{1,0:T(8,128)(2,1)} copy(bf16[512,2048]{1,0:T(8,128)(2,1)} %get-tuple-element.64) | data formatting | bytes 4194304
Async XLA Ops:
  0.0 205.3 %copy-start = (f32[512,2]{0,1:T(2,128)S(1)}, f32[512,2]{0,1:T(2,128)}, u32[]{:S(2)}) copy-start(f32[512,2]{0,1:T(2,128)} %param.18) | copy-start | bytes 12292
where the time goes:
time: 283 us
  Pallas kernels  278 us (98%)
  local copies, waits for them, and re-layouts  3.16 us (1%)
    pallas_call x1, Pallas kernels, front(): pl.pallas_call(functools.partial(front_kernel, cp_size, tp_size, heads, h...  204 us
    pallas_call x1, Pallas kernels, experts(): pl.pallas_call(functools.partial(moe_kernel, num_devs, tp_size, exp_local...  74.1 us

commit v1 on v0

--- a/solution.py
+++ b/solution.py
@@ -358,7 +358,7 @@
     await_bytes(kv_ref.at[pl.ds(0, tp_size * rows)], kv_send)
 
 
-def moe_kernel(num_devs, tp_size, exp_local, cap, full, tok_ref, h_ref, slot_ref, slots_ref, gate_ref, wg_ref, wu_ref, wd_ref, y_ref, tok, wgb, wub, wdb, zrecv, over, yacc, cols, tsem, wsem, send_sem, over_sem, recv_sem):
+def moe_kernel(num_devs, tp_size, exp_local, cap, full, tok_ref, h_ref, slot_ref, slots_ref, gate_ref, wg_ref, wu_ref, wd_ref, y_ref, tok, wgb, wub, wdb, zrecv, over, cols, tsem, wsem, send_sem, over_sem, recv_sem):
     rows, width = y_ref.shape
     r, t = lax.axis_index('cp'), lax.axis_index('tp')
     me = r * tp_size + t
@@ -390,7 +390,7 @@
     back = jnp.where(pos < low, home, upper)
     columns = jnp.concatenate([back.astype(jnp.float32), gate_ref[...], jnp.zeros((124, rows), jnp.float32)], axis=0)
     cols[...] = jnp.transpose(columns)
-    yacc[...] = h_ref[...].astype(jnp.float32)
+    y_ref[...] = h_ref[...].astype(jnp.float32)
     loads[0].wait()
 
     def send(src, dst, sem, group, n):
@@ -466,11 +466,10 @@
             z = zrecv[pl.ds(first, 2), :, c0:c0 + 512].reshape(span, 512)
             z0 = jnp.dot(sel0, z, preferred_element_type=jnp.float32)
             z1 = jnp.dot(sel1, z, preferred_element_type=jnp.float32)
-            yacc[:, c0:c0 + 512] += cols[:, 2:3] * z0 + cols[:, 3:4] * z1
+            y_ref[:, c0:c0 + 512] += cols[:, 2:3] * z0 + cols[:, 3:4] * z1
         return carry
 
     lax.fori_loop(0, groups, combine, 0)
-    y_ref[...] = yacc[...].astype(y_ref.dtype)
     await_bytes(tok.at[pl.ds(0, pairs), pl.ds(0, (num_devs - 1) * cap)], send_sem)
     await_bytes(tok.at[pl.ds(0, pairs if full else 2), pl.ds(0, (num_devs - 1) * cap)], over_sem)
 
@@ -522,8 +521,8 @@
             functools.partial(moe_kernel, num_devs, tp_size, exp_local, cap, full),
             in_specs=[hbm, vmem, vmem, vmem, vmem, hbm, hbm, hbm],
             out_specs=vmem,
-            out_shape=jax.ShapeDtypeStruct((rows, width), bf16),
-            scratch_shapes=[v16(exp_local, block, width), v16(2, width, ff), v16(2, width, ff), v16(2, ff, width), v16(blocks, block, width), v16(num_devs, OV, width), pltpu.VMEM((rows, width), f32), pltpu.VMEM((rows, 128), f32), dma((2,)), dma((3, 2)), dma, dma, dma((blocks // 2,))],
+            out_shape=jax.ShapeDtypeStruct((rows, width), f32),
+            scratch_shapes=[v16(exp_local, block, width), v16(2, width, ff), v16(2, width, ff), v16(2, ff, width), v16(blocks, block, width), v16(num_devs, OV, width), pltpu.VMEM((rows, 128), f32), dma((2,)), dma((3, 2)), dma, dma, dma((blocks // 2,))],
             compiler_params=params(2 if full else 1),
             name='moe_full' if full else 'moe',
         )(tok, h_own, own_slots, slots, gates, w_gate, w_up, w_down)
@@ -538,6 +537,7 @@
         flat = lambda w: w.reshape(width, -1)
         _, tok, h_own, own_slots, slots = front(x_blk, idx_blk.T, w_q, flat(w_k), flat(w_v), w_o.reshape(heads * head_dim, width), heads, head_dim, exp_local, capacity)
         few = jnp.max(slots[:, 4, 0]) <= LIMIT
-        return lax.cond(few, functools.partial(experts, False, capacity), functools.partial(experts, True, capacity), tok, h_own, own_slots, slots, gate_blk.T, w_gate, w_up, w_down)
+        total = lax.cond(few, functools.partial(experts, False, capacity), functools.partial(experts, True, capacity), tok, h_own, own_slots, slots, gate_blk.T, w_gate, w_up, w_down)
+        return total.astype(bf16)
 
     return jax.shard_map(device_fn, mesh=mesh, in_specs=(row_spec, head_spec, head_spec, head_spec, wo_spec, row_spec, row_spec, expert_spec, expert_spec, expert_spec), out_specs=row_spec, check_vma=False)

time: 283 us -> 284 us (level)
  no operation moved by 1% of the time
where the time goes in v1:
time: 284 us
  Pallas kernels  279 us (98%)
  other arithmetic  3.14 us (1%)
    pallas_call x1, Pallas kernels, front(): pl.pallas_call(functools.partial(front_kernel, cp_size, tp_size, heads, h...  204 us
    pallas_call x1, Pallas kernels, experts(): pl.pallas_call(functools.partial(moe_kernel, num_devs, tp_size, exp_local...  74.5 us

profile of v1, /device:TPU:0, one launch (start us, length us, event | category | flops | bytes accessed | tf_op | source)
XLA Modules:
  0.0 283.7 jit_solution(15598176062283213)
XLA Ops:
  0.0 0.0 copy-start.1
  0.0 204.0 %front.1 = (bf16[4096,2048]{1,0:T(8,128)(2,1)}, bf16[16,128,2048]{2,1,0:T(8,128)(2,1)}, bf16[512,2048]{1,0:T(8,128)(2,1)S(1)}, s32[8,512]{1,0:T(8,128)S(1)}, s32[8,8,512]{2,1,0:T(8,128)S(1)}) custom-call(bf16[512,2048]{1,0:T(8,128)(2,1)} %x_ref.1, s32[2,512]{1,0:T(2,128)} %bitcast.10, bf16[2048,8,128]{2,1,0:T(8,128)(2,1)} %wq_ref.1, ...), custom_call_target="tpu_custom_call" | custom-call | tf_op jit(solution)/shard_map/front/pallas_call | solution.py:499
  204.0 0.6 slice_reduce_fusion
  205.3 0.0 copy-done.1
  205.3 77.0 %conditional.6 = (bf16[512,2048]{1,0:T(8,128)(2,1)S(1)}) conditional(s32[]{:T(128)} %convert_element_type.12, (bf16[16,128,2048]{2,1,0:T(8,128)(2,1)}, bf16[512,2048]{1,0:T(8,128)(2,1)S(1)}, s32[8,512]{1,0:T(8,128)S(1)}, s32[8,8,512]{2,1,0:T(8,128)S(1)}, f32[2,512]{1,0:T(2,128)S(1)}, /*index=5*/bf16[16,2048,768]{2,1,0:T(8,128)(2,1)}, ...), branch_computations={%region_1.0_spmd, %region_2.0_spmd} | conditional | flops 1048576 | bytes 6291464
  205.4 74.5 %moe.1 = f32[512,2048]{1,0:T(8,128)} custom-call(bf16[16,128,2048]{2,1,0:T(8,128)(2,1)} %get-tuple-element.54.tok_ref, bf16[512,2048]{1,0:T(8,128)(2,1)S(1)} %get-tuple-element.55.h_ref, s32[8,512]{1,0:T(8,128)S(1)} %get-tuple-element.56.slot_ref, s32[8,8,512]{2,1,0:T(8,128)S(1)} %get-tuple-element.57.slots_ref, f32[2,512]{1,0:T(2,128)S(1)} %get-tuple-element.58.gate_ref, ...), custom_call_target="tpu_custom_call" | custom-call | tf_op jit(solution)/shard_map/cond/branch_1_fun/moe/pallas_call | solution.py:520
  279.9 2.5 convert.1
  282.4 0.0 copy-start
  282.4 1.3 copy-done
Async XLA Ops:
  0.0 205.3 %copy-start.1 = (f32[512,2]{0,1:T(2,128)S(1)}, f32[512,2]{0,1:T(2,128)}, u32[]{:S(2)}) copy-start(f32[512,2]{0,1:T(2,128)} %param.18) | copy-start | bytes 12292
  282.4 1.3 copy-start
